TPU v7x, 32 devices: a whole 2x2x4 slice. The times are simulated.
32 devices in a mesh: rows: 8 (over z, x), bal: 4 (over y, core).
Axes of the slice: x: 2, y: 2, z: 4, core: 2. Of those that a mesh axis runs over, the one named last changes fastest.
Arguments:
- embeddings: bfloat16 [16384, 1024], P(('rows', 'bal')), may hold values from -60 to 60
- cluster_blocks: int32 [16], replicated, may hold values from 1 to 4, as said below
Outputs:
- row_max: float32 [16384], P(('rows', 'bal'))
Inputs may be any that keep to these rules, and one draw needn't show every extreme that they name: `cluster_blocks`: the sizes sum to 32; at least one cluster has exactly 4 blocks.
All inputs are finite; a program needn't handle non-finite values.
Results may differ from a plain program's by a relative error of at most 0.00051.
Values may be sent and summed in bfloat16 or wider, within the bound.
A program may use at most 64 MiB of HBM per device.

v0:
```python
import functools

import jax
import jax.numpy as jnp
from jax import lax
from jax.experimental import pallas as pl
from jax.experimental.pallas import tpu as pltpu
from jax.sharding import PartitionSpec as P

EPSILON = 1e-06
LOW = -2.0
MESH_ID = pl.DeviceIdType.MESH
PIECES = 8


def nearest_kernel(sizes, counts_hbm, x_ref, out_ref, raw, pair, two_back, three_back,
                   row_two, row_three, best, part_out, ret_out, ret3_out, part_in, ret_in, ret3_in,
                   load_sem, pair_send, pair_recv, two_send, two_recv, three_send, three_recv,
                   small_send, small_recv, counts_ref, counts_sem):
    n_rows, n_bal = sizes
    total = n_rows * n_bal
    block, width = x_ref.shape
    piece = block // PIECES
    me = lax.axis_index("rows") * n_bal + lax.axis_index("bal")
    odd = lax.rem(me, 2)
    quarter = lax.rem(me, 4)
    partner = me + 1 - 2 * odd
    is_even = odd == 0
    is_odd = odd == 1

    has_later = me + 2 < total
    has_earlier = me >= 2
    has_later3 = is_odd & (me + 3 < total)
    has_earlier3 = is_even & (me >= 3)
    sends_direct = has_later & ((quarter != 3) | (me + 3 >= total))
    relays = has_earlier3 & (quarter == 2)
    relayed_to = has_earlier & (quarter == 1) & (me + 1 < total)

    def coords(index):
        return (index // n_bal, lax.rem(index, n_bal))

    barrier = pltpu.get_barrier_semaphore()
    greeted = jnp.int32(0)
    for there, index in (
        (me >= 0, partner),
        (has_later, me + 2),
        (has_earlier, me - 2),
        (has_later3, me + 3),
        (has_earlier3, me - 3),
        (relays, me - 1),
        (relayed_to, me + 1),
    ):
        @pl.when(there)
        def _():
            pl.semaphore_signal(barrier, inc=1, device_id=coords(index), device_id_type=MESH_ID)
        greeted = greeted + there.astype(jnp.int32)

    def load(q):
        rows = pl.ds(pl.multiple_of(q * piece, piece), piece)
        return pltpu.make_async_copy(x_ref.at[rows], raw.at[rows], load_sem.at[q])

    @pl.loop(0, PIECES)
    def _(q):
        load(q).start()

    counts_load = pltpu.make_async_copy(counts_hbm, counts_ref, counts_sem)
    counts_load.start()


    @pl.loop(0, PIECES)
    def _(q):
        rows = pl.ds(pl.multiple_of(q * piece, piece), piece)
        load(q).wait()
        values = raw[rows, :].astype(jnp.float32)
        scale = lax.rsqrt(jnp.sum(values * values, axis=1, keepdims=True) + EPSILON)
        pair[0, rows, :] = (values * scale).astype(jnp.bfloat16)

    pl.semaphore_wait(barrier, greeted)

    def rows_of(q):
        return pl.ds(pl.multiple_of(q * piece, piece), piece)

    def to_two(q):
        return pltpu.make_async_remote_copy(
            src_ref=pair.at[0, rows_of(q)], dst_ref=two_back.at[rows_of(q)],
            send_sem=two_send.at[q], recv_sem=two_recv.at[q],
            device_id=coords(me + 2), device_id_type=MESH_ID)

    def to_three(q):
        return pltpu.make_async_remote_copy(
            src_ref=pair.at[0, rows_of(q)], dst_ref=three_back.at[rows_of(q)],
            send_sem=three_send.at[q], recv_sem=three_recv.at[q],
            device_id=coords(me + 3), device_id_type=MESH_ID)

    def onward(q):
        return pltpu.make_async_remote_copy(
            src_ref=three_back.at[rows_of(q)], dst_ref=two_back.at[rows_of(q)],
            send_sem=three_send.at[q], recv_sem=two_recv.at[q],
            device_id=coords(me - 1), device_id_type=MESH_ID)

    def to_partner():
        return pltpu.make_async_remote_copy(
            src_ref=pair.at[0], dst_ref=pair.at[1],
            send_sem=pair_send, recv_sem=pair_recv,
            device_id=coords(partner), device_id_type=MESH_ID)

    def small(slot, src, dst, index):
        return pltpu.make_async_remote_copy(
            src_ref=src, dst_ref=dst, send_sem=small_send.at[slot], recv_sem=small_recv.at[slot],
            device_id=coords(index), device_id_type=MESH_ID)

    to_partner().start()

    @pl.loop(0, PIECES)
    def _(q):
        @pl.when(has_later3)
        def _():
            to_three(q).start()

        @pl.when(sends_direct)
        def _():
            to_two(q).start()

    counts_load.wait()

    def count(i, carry):
        end, crossings = carry
        end = end + counts_ref[i]
        found = []
        for (lower, upper), old in zip(spans, crossings):
            found.append(old + ((end > lower) & (end <= upper)).astype(jnp.int32))
        return end, tuple(found)

    spans = ((me - 3, me), (me - 2, me), (me - 1, me), (me, me + 1), (me - 2, partner))
    zero = jnp.int32(0)
    _, crossings = lax.fori_loop(0, counts_ref.shape[0], count, (zero, (zero,) * len(spans)))
    near3 = crossings[0] == 0
    near2 = crossings[1] == 0
    near_partner = jnp.where(is_odd, crossings[2], crossings[3]) == 0
    near2_partner = crossings[4] == 0

    def products(left, right):
        return lax.dot_general(left, right, (((1,), (1,)), ((), ())),
                               preferred_element_type=jnp.float32)

    step = 128
    best[...] = jnp.full(best.shape, LOW, jnp.float32)

    @pl.loop(0, block // step)
    def _(s):
        rows = pl.ds(pl.multiple_of(s * step, step), step)
        own = products(pair[0, rows, :], pair[0])
        across = lax.broadcasted_iota(jnp.int32, own.shape, 1)
        down = lax.broadcasted_iota(jnp.int32, own.shape, 0) + s * step
        own = jnp.where(across == down, LOW, own)
        best[0:1, :] = jnp.maximum(best[0:1, :], jnp.max(own, axis=0, keepdims=True))

    to_partner().wait()

    @pl.loop(0, block // step)
    def _(s):
        rows = pl.ds(pl.multiple_of(s * step, step), step)
        other = products(pair[1, rows, :], pair[0])
        top = jnp.max(other, axis=0, keepdims=True)
        best[0:1, :] = jnp.maximum(best[0:1, :], jnp.where(near_partner, top, LOW))

    def lanes_max(tile):
        highest = tile[:, :128]
        for start in range(128, tile.shape[1], 128):
            highest = jnp.maximum(highest, tile[:, start:start + 128])
        return highest

    @pl.loop(0, PIECES)
    def _(q):
        rows = rows_of(q)

        @pl.when(has_earlier3)
        def _():
            to_three(q).wait_recv()

            @pl.when(relays)
            def _():
                onward(q).start()

            tile = products(three_back[rows, :], pair[0])
            row_three[rows, :] = lanes_max(tile)
            top = jnp.max(tile, axis=0, keepdims=True)
            best[0:1, :] = jnp.maximum(best[0:1, :], jnp.where(near3, top, LOW))

        @pl.when(has_earlier)
        def _():
            to_two(q).wait_recv()
            tile = products(two_back[rows, :], pair[0])
            other = products(two_back[rows, :], pair[1])
            row_two[rows, :] = jnp.maximum(
                jnp.where(near2, lanes_max(tile), LOW),
                jnp.where(near2_partner, lanes_max(other), LOW))
            top = jnp.max(tile, axis=0, keepdims=True)
            best[0:1, :] = jnp.maximum(best[0:1, :], jnp.where(near2, top, LOW))
            top = jnp.max(other, axis=0, keepdims=True)
            best[1:2, :] = jnp.maximum(best[1:2, :], jnp.where(near2_partner, top, LOW))

    @pl.when(has_earlier)
    def _():
        ret_out[...] = jnp.max(row_two[...].T, axis=0, keepdims=True)
        part_out[...] = best[1:2, :]
        small(0, ret_out, ret_in, me - 2).start()
        small(1, part_out, part_in, partner).start()

    @pl.when(has_earlier3)
    def _():
        top = jnp.max(row_three[...].T, axis=0, keepdims=True)
        ret3_out[...] = jnp.where(near3, top, LOW)
        small(2, ret3_out, ret3_in, me - 3).start()

    @pl.when(has_earlier)
    def _():
        small(1, part_out, part_in, partner).wait()
        best[0:1, :] = jnp.maximum(best[0:1, :], part_in[...])

    @pl.when(has_later3)
    def _():
        small(2, ret3_out, ret3_in, me + 3).wait_recv()
        best[0:1, :] = jnp.maximum(best[0:1, :], ret3_in[...])

    @pl.when(has_later)
    def _():
        small(0, ret_out, ret_in, me + 2).wait_recv()
        best[0:1, :] = jnp.maximum(best[0:1, :], ret_in[...])

    out_ref[...] = best[0:1, :]

    @pl.loop(0, PIECES)
    def _(q):
        @pl.when(has_later3)
        def _():
            to_three(q).wait_send()

        @pl.when(sends_direct)
        def _():
            to_two(q).wait_send()

        @pl.when(relays)
        def _():
            onward(q).wait_send()

    @pl.when(has_earlier)
    def _():
        small(0, ret_out, ret_in, me - 2).wait_send()

    @pl.when(has_earlier3)
    def _():
        small(2, ret3_out, ret3_in, me - 3).wait_send()


def shards(sizes, embeddings, cluster_blocks):
    block, width = embeddings.shape
    line = pltpu.VMEM((1, block), jnp.float32)
    wide = pltpu.VMEM((block, width), jnp.bfloat16)
    flags = pltpu.SemaphoreType.DMA((PIECES,))
    lone = pltpu.SemaphoreType.DMA
    out = pl.pallas_call(
        functools.partial(nearest_kernel, sizes),
        out_shape=pltpu.VMEM((1, block), jnp.float32),
        in_specs=[pl.BlockSpec(memory_space=pl.ANY)] * 2,
        out_specs=pl.BlockSpec(memory_space=pltpu.VMEM),
        scratch_shapes=[
            wide, pltpu.VMEM((2, block, width), jnp.bfloat16), wide, wide,
            pltpu.VMEM((block, 128), jnp.float32), pltpu.VMEM((block, 128), jnp.float32),
            pltpu.VMEM((8, block), jnp.float32),
            line, line, line, line, line, line,
            flags, lone, lone, flags, flags, flags, flags,
            pltpu.SemaphoreType.DMA((3,)), pltpu.SemaphoreType.DMA((3,)),
            pltpu.SMEM(cluster_blocks.shape, jnp.int32), lone,
        ],
        compiler_params=pltpu.CompilerParams(collective_id=0, has_side_effects=True),
        name="nearest",
    )(cluster_blocks, embeddings)
    return out.reshape(-1)


def solution(mesh):
    sizes = (mesh.shape["rows"], mesh.shape["bal"])
    return jax.shard_map(
        functools.partial(shards, sizes), mesh=mesh,
        in_specs=(P(("rows", "bal"), None), P()), out_specs=P(("rows", "bal")), check_vma=False)
```

profile of v0, /device:TPU:7, one launch (start us, length us, event | category | flops | bytes accessed | tf_op | source)
XLA Modules:
  0.0 34.2 jit_solution(91923784879084338)
XLA Ops:
  0.0 33.6 %nearest.1 = f32[1,512]{1,0:T(1,128)S(1)} custom-call(s32[16]{0:T(128)} %counts_hbm.1, bf16[512,1024]{1,0:T(8,128)(2,1)} %x_ref.1), custom_call_target="tpu_custom_call" | custom-call | tf_op jit(solution)/shard_map/nearest/pallas_call | solution.py:262
  33.6 0.6 %copy.4 = f32[512]{0:T(512)} copy(f32[512]{0:T(512)S(1)} %bitcast.1) | data formatting | bytes 4096
where the time goes:
time: 34.4 us; the launch traced here: 34.2 us
  Pallas kernels  33.6 us (98%)
  local copies, waits for them, and re-layouts  0.58 us (2%)
    pallas_call x1, Pallas kernels, shards(): pl.pallas_call(functools.partial(nearest_kernel, sizes), out_shape=pltpu....  33.6 us

commit v1 on v0

v1 whole, which is shorter than its diff:
```python
import functools

import jax
import jax.numpy as jnp
from jax import lax
from jax.experimental import pallas as pl
from jax.experimental.pallas import tpu as pltpu
from jax.sharding import PartitionSpec as P

EPSILON = 1e-06
LOW = -2.0
MESH_ID = pl.DeviceIdType.MESH
PIECES = 8
HALF = PIECES // 2
GROUP = 8

NEAR = ((0, 1), (0, 2), (0, 3), (0, 5), (0, 6), (0, 7), (1, 2), (1, 4), (2, 3), (2, 4), (2, 6),
        (3, 5), (3, 6), (4, 5), (4, 6), (5, 6), (5, 7), (6, 7))
ACROSS = ((0, 0), (0, 1), (5, 0), (5, 1), (5, 4), (7, 1), (7, 2), (7, 6))
MAIN_OFFSET = (-8, 1, -2, 3, 2, -5, -1, 7)
MAIN_SLOT = (2, 0, 0, 1, 0, 1, 0, 2)
FIRST_SEEN, LAST_SEEN = -1, 9


def nearest_kernel(sizes, counts_hbm, x_ref, out_ref, raw, own, other, wide_in, stage, acc, *rest):
    rest = list(rest)

    def several(many):
        return [rest.pop(0) for _ in range(many)]

    main_in, half_in, ret_in, lines = several(3), several(2), several(5), [None] + several(6)
    main_recv, half_recv, side_send = several(3), several(2), several(3)
    (load_sem, pair_send, pair_recv, main_send, wide_recv, ret_send, ret_recv,
     counts_ref, counts_sem) = rest
    n_rows, n_bal = sizes
    total = n_rows * n_bal
    block, width = x_ref.shape
    piece = block // PIECES
    tile = 2 * piece
    half = block // 2
    me = lax.axis_index("rows") * n_bal + lax.axis_index("bal")
    role = lax.rem(me, GROUP)
    base = me - role
    has_up = base + GROUP < total
    has_down = base > 0
    partner = me + 1 - 2 * lax.rem(me, 2)

    def coords(index):
        return (index // n_bal, lax.rem(index, n_bal))

    def by_role(values):
        return sum((role == place).astype(jnp.int32) * value for place, value in enumerate(values))

    barrier = pltpu.get_barrier_semaphore()
    near_of = [[b if a == r else a for a, b in NEAR if r in (a, b)] for r in range(GROUP)]
    up_of = [[b for a, b in ACROSS if a == r] for r in range(GROUP)]
    down_of = [[a for a, b in ACROSS if b == r] for r in range(GROUP)]

    def greet(index):
        pl.semaphore_signal(barrier, inc=1, device_id=coords(index), device_id_type=MESH_ID)

    for r in range(GROUP):
        @pl.when(role == r)
        def _():
            @pl.when(has_up)
            def _():
                for there in up_of[r]:
                    greet(me + GROUP + there - r)

            @pl.when(has_down)
            def _():
                for there in down_of[r]:
                    greet(me - GROUP + there - r)

            for there in near_of[r]:
                greet(me + there - r)

    greeted = (by_role([len(n) for n in near_of])
               + has_up.astype(jnp.int32) * by_role([len(n) for n in up_of])
               + has_down.astype(jnp.int32) * by_role([len(n) for n in down_of]))

    def rows_of(q, size=piece):
        return pl.ds(pl.multiple_of(q * size, size), size)

    def load(q):
        return pltpu.make_async_copy(x_ref.at[rows_of(q)], raw.at[rows_of(q)], load_sem.at[q])

    counts_load = pltpu.make_async_copy(counts_hbm, counts_ref, counts_sem)
    counts_load.start()

    @pl.loop(0, PIECES)
    def _(q):
        load(q).start()

    def copy_to(src, dst, send, recv, index):
        return pltpu.make_async_remote_copy(
            src_ref=src, dst_ref=dst, send_sem=send, recv_sem=recv,
            device_id=coords(index), device_id_type=MESH_ID)

    def to_main(r, q):
        slot = MAIN_SLOT[r]
        return copy_to(own.at[rows_of(q)], main_in[slot].at[rows_of(q)],
                       main_send.at[q], main_recv[slot].at[q], me + MAIN_OFFSET[r])

    def for_main(act):
        for r in range(GROUP):
            here = role == r
            if r == 0:
                here = here & has_down
            if r == 7:
                here = here & has_up
            pl.when(here)(functools.partial(act, r))

    def to_pair(q):
        return copy_to(own.at[rows_of(q)], other.at[rows_of(q)], pair_send.at[q], pair_recv.at[q], partner)

    def side(slot, q, src, dst, recv, index):
        return copy_to(src, dst, side_send[slot].at[q], recv, index)

    def high_half(q):
        low = q - HALF
        return side(0, low, own.at[rows_of(q)], half_in[0].at[rows_of(low)], half_recv[0].at[low], me - 7)

    def normalise(q):
        rows = rows_of(q)
        load(q).wait()
        values = raw[rows, :].astype(jnp.float32)
        scale = lax.rsqrt(jnp.sum(values * values, axis=1, keepdims=True) + EPSILON)
        own[rows, :] = (values * scale).astype(jnp.bfloat16)

    def send(q):
        for_main(lambda r: to_main(r, q).start())

        @pl.when((role == 7) & (q >= HALF))
        def _():
            high_half(q).start()

        to_pair(q).start()

    pl.loop(0, HALF)(normalise)
    pl.semaphore_wait(barrier, greeted)
    pl.loop(0, HALF)(send)

    @pl.loop(HALF, PIECES)
    def _(q):
        normalise(q)
        send(q)

    counts_load.wait()

    def count(i, carry):
        end, owners = carry
        end = end + counts_ref[i]
        return end, tuple(
            owner + (end <= base + place).astype(jnp.int32)
            for place, owner in zip(range(FIRST_SEEN, LAST_SEEN + 1), owners))

    zero = jnp.int32(0)
    _, owners = lax.fori_loop(0, counts_ref.shape[0], count,
                              (zero, (zero,) * (LAST_SEEN + 1 - FIRST_SEEN)))

    def same(i, j):
        return owners[i - FIRST_SEEN] == owners[j - FIRST_SEEN]

    whole = same(0, 3)
    below = same(-1, 2) & has_down
    acc[...] = jnp.full(acc.shape, LOW, jnp.float32)

    def products(left, right):
        return lax.dot_general(left, right, (((1,), (1,)), ((), ())),
                               preferred_element_type=jnp.float32)

    def lanes_max(values):
        highest = values[:, :128]
        for start in range(128, values.shape[1], 128):
            highest = jnp.maximum(highest, values[:, start:start + 128])
        return highest

    def raise_to(slot, lanes, top):
        acc[slot, :, lanes] = jnp.maximum(acc[slot, :, lanes], top)

    everywhere = slice(None)
    low_lanes = slice(0, half)
    high_lanes = slice(half, block)

    def meet(left, partners, row_slot, p, shift=0):
        part = None
        for right, permitted, column_slot, lanes in partners:
            values = products(left, right)
            top = jnp.max(values, axis=0, keepdims=True)
            raise_to(column_slot, lanes, jnp.where(permitted, top, LOW))
            across = jnp.where(permitted, lanes_max(values), LOW)
            part = across if part is None else jnp.maximum(part, across)
        lanes = pl.ds(pl.multiple_of(p * tile + shift, tile), tile)
        raise_to(row_slot, lanes, jnp.max(part.T, axis=0, keepdims=True))

    def diagonal():
        @pl.loop(0, block // tile)
        def _(p):
            values = products(own[rows_of(p, tile), :], own[...])
            across = lax.broadcasted_iota(jnp.int32, values.shape, 1)
            down = lax.broadcasted_iota(jnp.int32, values.shape, 0) + p * tile
            values = jnp.where(across == down, LOW, values)
            raise_to(0, everywhere, jnp.max(values, axis=0, keepdims=True))

    def pair_tile(permitted):
        @pl.loop(0, block // tile)
        def _(p):
            meet(other[rows_of(p, tile), :], [(own[...], permitted, 0, everywhere)], 1, p)

    def wait_pair(begin=0, end=PIECES):
        @pl.loop(begin, end)
        def _(q):
            to_pair(q).wait_recv()

    def wait_main(slot, q):
        copy_to(own.at[rows_of(q)], main_in[slot].at[rows_of(q)],
                main_send.at[q], main_recv[slot].at[q], me).wait_recv()

    def wait_wide(q):
        side(0, q, stage.at[rows_of(q)], wide_in.at[rows_of(q)], wide_recv.at[q], me).wait_recv()

    def wait_half(slot, q):
        side(0, q, stage.at[rows_of(q)], half_in[slot].at[rows_of(q)], half_recv[slot].at[q], me).wait_recv()

    def both(wait, p):
        wait(2 * p)
        wait(2 * p + 1)

    def ret(slot, offset, place):
        return copy_to(lines[max(slot, 1)], ret_in[place], ret_send.at[slot], ret_recv.at[place], me + offset)

    def give(slot, offset, place):
        lines[slot][...] = acc[slot]
        ret(slot, offset, place).start()

    tiles = block // tile
    half_tiles = half // tile

    def split(slot, chosen, first_slot, first_lanes, second_slot, second_lanes, lanes):
        acc[first_slot, :, first_lanes] = jnp.where(chosen, acc[slot, :, lanes], LOW)
        acc[second_slot, :, second_lanes] = jnp.where(chosen, LOW, acc[slot, :, lanes])

    def zero_side(q):
        return side(0, q, stage.at[rows_of(q)], half_in[0].at[rows_of(q)], half_recv[0].at[q], me + 3)

    def zero_relay(q):
        return side(1, q, main_in[2].at[rows_of(q)], wide_in.at[rows_of(q)], wide_recv.at[q], me + 5)

    def zero_down(q):
        return side(2, q, other.at[rows_of(q + HALF)], half_in[1].at[rows_of(q)], half_recv[1].at[q], me - 8)

    @pl.when(role == 0)
    def _():
        wait_pair()

        @pl.when(has_down)
        def _():
            @pl.loop(0, HALF)
            def _(q):
                zero_down(q).start()

        diagonal()

        def pass_on(q):
            @pl.when(has_up)
            def _():
                wait_main(2, q)
                zero_relay(q).start()

        @pl.loop(0, HALF)
        def _(q):
            rows = rows_of(q)
            wait_main(1, q)
            stage[rows, :] = jnp.where(whole, own[rows_of(q + HALF), :], main_in[1][rows, :])
            zero_side(q).start()
            pass_on(q)

        @pl.loop(HALF, PIECES)
        def _(q):
            wait_main(1, q)
            pass_on(q)

        @pl.loop(0, half_tiles)
        def _(p):
            both(lambda q: wait_half(0, q), p)
            left = half_in[0][rows_of(p, tile), :]
            meet(left, [(main_in[1][...], same(5, 7), 2, everywhere)], 3, p, half)

            @pl.when(has_up)
            def _():
                meet(left, [(main_in[2][...], same(7, 8), 4, everywhere)], 3, p, half)

        @pl.loop(0, tiles)
        def _(p):
            both(lambda q: wait_main(0, q), p)
            meet(main_in[0][rows_of(p, tile), :],
                 [(own[...], same(0, 2), 0, everywhere), (main_in[1][...], same(2, 5), 2, everywhere)], 1, p)

        give(1, 2, 0)
        give(2, 5, 1)

        @pl.when(has_up)
        def _():
            @pl.loop(0, half_tiles)
            def _(p):
                both(lambda q: wait_half(1, q), p)
                meet(half_in[1][rows_of(p, tile), :], [(half_in[0][...], same(7, 9), 3, high_lanes)], 5, p, half)

            give(4, 8, 4)
            give(5, 9, 2)

        give(3, 7, 2)

    def one_side(q):
        return side(0, q, stage.at[rows_of(q)], half_in[0].at[rows_of(q)], half_recv[0].at[q], me + 3)

    @pl.when(role == 1)
    def _():
        @pl.loop(0, HALF)
        def _(q):
            to_pair(q).wait_recv()
            rows = rows_of(q)
            stage[rows, :] = jnp.where(whole, other[rows, :], own[rows_of(q + HALF), :])
            one_side(q).start()

        diagonal()
        wait_pair(HALF, PIECES)
        pair_tile(same(0, 1))
        give(1, -1, 0)

    def two_down(q):
        return side(0, q, main_in[0].at[rows_of(q)], half_in[0].at[rows_of(q)], half_recv[0].at[q], me - 3)

    @pl.when(role == 2)
    def _():
        wait_pair()
        diagonal()
        from_four = same(1, 4) & jnp.logical_not(below)

        @pl.loop(0, HALF)
        def _(q):
            wait_main(0, q)

            @pl.when(has_down)
            def _():
                two_down(q).start()

        def first_block(p):
            meet(main_in[0][rows_of(p, tile), :],
                 [(own[...], same(1, 2), 0, everywhere), (other[...], same(1, 3), 2, everywhere)], 1, p)

        pl.loop(0, half_tiles)(first_block)

        def chosen_block(p):
            both(wait_wide, p)
            meet(wide_in[rows_of(p, tile), :],
                 [(own[...], below | same(2, 4), 0, everywhere),
                  (main_in[0][:half, :], from_four, 1, low_lanes)], 3, p)

        pl.loop(0, half_tiles)(chosen_block)

        @pl.loop(half_tiles, tiles)
        def _(p):
            both(lambda q: wait_main(0, q), p)
            first_block(p)

        give(2, 1, 0)
        pl.loop(half_tiles, tiles)(chosen_block)

        @pl.loop(half_tiles, tiles)
        def _(p):
            meet(main_in[0][rows_of(p, tile), :], [(wide_in[...], from_four, 3, everywhere)], 1, p)

        split(3, below, 5, everywhere, 4, everywhere, everywhere)
        give(1, -1, 0)
        give(4, 2, 1)

        @pl.when(has_down)
        def _():
            give(5, -3, 3)

    @pl.when(role == 3)
    def _():
        wait_pair()
        diagonal()
        pair_tile(same(2, 3))
        give(1, -1, 1)

        @pl.loop(0, half_tiles)
        def _(p):
            both(lambda q: wait_half(0, q), p)
            meet(half_in[0][rows_of(p, tile), :], [(own[...], whole | same(3, 5), 0, everywhere)], 2, p)

        split(2, whole, 3, high_lanes, 4, low_lanes, low_lanes)
        give(3, -3, 1)
        give(4, 2, 2)

    def four_side(q):
        return side(0, q, stage.at[rows_of(q)], half_in[0].at[rows_of(q)], half_recv[0].at[q], me + 2)

    def four_down(q):
        return side(1, q, half_in[0].at[rows_of(q)], half_in[1].at[rows_of(q)], half_recv[1].at[q], me - 7)

    @pl.when(role == 4)
    def _():
        wait_pair()
        diagonal()

        @pl.loop(0, HALF)
        def _(q):
            wait_half(0, q)

            @pl.when(has_down)
            def _():
                four_down(q).start()

            rows = rows_of(q)
            stage[rows, :] = jnp.where(whole, half_in[0][rows, :], other[rows_of(q + HALF), :])
            four_side(q).start()

        pair_tile(same(4, 5))
        give(1, 1, 0)

    @pl.when(role == 5)
    def _():
        wait_pair()
        diagonal()

        @pl.loop(0, tiles)
        def _(p):
            both(lambda q: wait_main(0, q), p)
            meet(main_in[0][rows_of(p, tile), :], [(own[...], same(5, 6), 0, everywhere)], 1, p)

        @pl.when(has_up)
        def _():
            @pl.loop(0, half_tiles)
            def _(p):
                both(lambda q: wait_half(1, q), p)
                meet(half_in[1][rows_of(p, tile), :], [(main_in[0][...], same(6, 9), 1, everywhere)], 4, p, half)

        @pl.loop(0, half_tiles)
        def _(p):
            @pl.when(has_up)
            def _():
                @pl.loop(2 * p, 2 * p + 2)
                def _(i):
                    both(wait_wide, i)
                    meet(wide_in[rows_of(i, tile), :],
                         [(own[...], same(5, 8), 0, everywhere), (main_in[0][...], same(6, 8), 1, everywhere)], 3, i)

            both(lambda q: wait_half(0, q), p)
            left = half_in[0][rows_of(p, tile), :]
            meet(left, [(own[...], same(5, 7), 0, everywhere)], 2, p)

            @pl.when(has_up)
            def _():
                meet(left, [(half_in[1][...], same(7, 9), 4, high_lanes)], 2, p)

        give(1, 1, 0)

        @pl.when(has_up)
        def _():
            @pl.loop(0, half_tiles)
            def _(p):
                meet(half_in[0][rows_of(p, tile), :], [(wide_in[...], same(7, 8), 3, everywhere)], 2, p)

            give(3, 3, 3)
            give(4, 4, 1)

        give(2, 2, 1)

    def six_side(q):
        return side(0, q, stage.at[rows_of(q)], wide_in.at[rows_of(q)], wide_recv.at[q], me - 4)

    def six_low(q):
        return side(1, q, other.at[rows_of(q)], half_in[0].at[rows_of(q)], half_recv[0].at[q], me - 1)

    @pl.when(role == 6)
    def _():
        wait_pair()

        @pl.loop(0, HALF)
        def _(q):
            six_low(q).start()

        diagonal()

        def choose(q):
            rows = rows_of(q)
            wait_main(0, q)

            @pl.when(has_down)
            def _():
                wait_main(2, q)
                stage[rows, :] = jnp.where(below, main_in[2][rows, :], main_in[0][rows, :])

            @pl.when(jnp.logical_not(has_down))
            def _():
                stage[rows, :] = main_in[0][rows, :]

            six_side(q).start()

        @pl.loop(0, tiles)
        def _(p):
            both(choose, p)
            meet(main_in[0][rows_of(p, tile), :],
                 [(own[...], same(4, 6), 0, everywhere), (other[...], same(4, 7), 2, everywhere)], 1, p)

        give(2, 1, 0)

        @pl.loop(0, tiles)
        def _(p):
            both(lambda q: wait_main(1, q), p)
            meet(main_in[1][rows_of(p, tile), :],
                 [(own[...], same(3, 6), 0, everywhere), (main_in[0][...], same(3, 4), 1, everywhere)], 3, p)

        give(1, -2, 0)

        @pl.loop(0, half_tiles)
        def _(p):
            both(lambda q: wait_half(0, q), p)
            meet(half_in[0][rows_of(p, tile), :], [(main_in[1][...], whole | same(3, 5), 3, everywhere)], 4, p)

        split(4, whole, 5, low_lanes, 6, high_lanes, low_lanes)
        give(3, -3, 1)
        give(5, -6, 2)
        give(6, -1, 3)

    @pl.when(role == 7)
    def _():
        wait_pair()
        diagonal()
        pair_tile(same(6, 7))

        @pl.when(has_up)
        def _():
            @pl.loop(0, half_tiles)
            def _(p):
                both(lambda q: wait_half(0, q), p)
                meet(half_in[0][rows_of(p, tile), :],
                     [(own[...], same(7, 9), 0, everywhere), (other[...], same(6, 9), 1, everywhere)], 2, p)

            give(2, 2, 3)

        give(1, -1, 1)

    def take(*places):
        for place in places:
            ret(0, 0, place).wait_recv()
            raise_to(0, everywhere, ret_in[place][...])

    expected = ((0, 1, 2), (0,), (0, 1), (0, 1), (0, 1), (0, 1, 2, 3), (0, 1), (0, 1, 2))
    for r in range(GROUP):
        @pl.when(role == r)
        def _():
            take(*expected[r])

    @pl.when(has_down & (role == 0))
    def _():
        take(3, 4)

    @pl.when(has_down & (role == 1))
    def _():
        take(1, 2, 3)

    @pl.when(has_up & (role == 7))
    def _():
        take(3)

    out_ref[...] = acc[0]

    @pl.loop(0, PIECES)
    def _(q):
        to_pair(q).wait_send()

        for_main(lambda r: to_main(r, q).wait_send())

        @pl.when((role == 0) & has_up)
        def _():
            zero_relay(q).wait_send()

        @pl.when(role == 6)
        def _():
            six_side(q).wait_send()

    @pl.loop(0, HALF)
    def _(q):
        @pl.when(role == 0)
        def _():
            zero_side(q).wait_send()

            @pl.when(has_down)
            def _():
                zero_down(q).wait_send()

        @pl.when(role == 1)
        def _():
            one_side(q).wait_send()

        @pl.when((role == 2) & has_down)
        def _():
            two_down(q).wait_send()

        @pl.when(role == 4)
        def _():
            four_side(q).wait_send()

            @pl.when(has_down)
            def _():
                four_down(q).wait_send()

        @pl.when(role == 6)
        def _():
            six_low(q).wait_send()

        @pl.when(role == 7)
        def _():
            high_half(q + HALF).wait_send()

    sent = ((1, 2, 3), (1,), (1, 2, 4), (1, 3, 4), (1,), (1, 2), (1, 2, 3, 5, 6), (1,))
    sent_up = ((4, 5), (), (), (), (), (3, 4), (), (2,))
    for r in range(GROUP):
        @pl.when(role == r)
        def _():
            for slot in sent[r]:
                ret(slot, 0, 0).wait_send()

            @pl.when(has_up)
            def _():
                for slot in sent_up[r]:
                    ret(slot, 0, 0).wait_send()

    @pl.when((role == 2) & has_down)
    def _():
        ret(5, 0, 0).wait_send()


def shards(sizes, embeddings, cluster_blocks):
    block, width = embeddings.shape
    wide = pltpu.VMEM((block, width), jnp.bfloat16)
    half = pltpu.VMEM((block // 2, width), jnp.bfloat16)
    line = pltpu.VMEM((1, block), jnp.float32)
    flags = pltpu.SemaphoreType.DMA((PIECES,))
    lone = pltpu.SemaphoreType.DMA
    out = pl.pallas_call(
        functools.partial(nearest_kernel, sizes),
        out_shape=pltpu.VMEM((1, block), jnp.float32),
        in_specs=[pl.BlockSpec(memory_space=pl.ANY)] * 2,
        out_specs=pl.BlockSpec(memory_space=pltpu.VMEM),
        scratch_shapes=[
            wide, wide, wide, wide, wide,
            pltpu.VMEM((8, 1, block), jnp.float32),
            wide, wide, wide, half, half, *[line] * 11, *[flags] * 8,
            flags, flags, flags, flags, flags,
            pltpu.SemaphoreType.DMA((7,)), pltpu.SemaphoreType.DMA((5,)),
            pltpu.SMEM(cluster_blocks.shape, jnp.int32), lone,
        ],
        compiler_params=pltpu.CompilerParams(collective_id=0, has_side_effects=True),
        name="nearest",
    )(cluster_blocks, embeddings)
    return out.reshape(-1)


def solution(mesh):
    sizes = (mesh.shape["rows"], mesh.shape["bal"])
    return jax.shard_map(
        functools.partial(shards, sizes), mesh=mesh,
        in_specs=(P(("rows", "bal"), None), P()), out_specs=P(("rows", "bal")), check_vma=False)
```

time: 34.4 us -> 29.4 us (0.85)
  the two profiles are of different devices: /device:TPU:7 before, /device:TPU:1 now
where the time goes in v1:
time: 29.4 us; the launch traced here: 29.1 us
  Pallas kernels  28.5 us (97%)
  local copies, waits for them, and re-layouts  0.58 us (2%)
    pallas_call x1, Pallas kernels, shards(): pl.pallas_call(functools.partial(nearest_kernel, sizes), out_shape=pltpu....  28.5 us

profile of v1, /device:TPU:1, one launch (start us, length us, event | category | flops | bytes accessed | tf_op | source)
XLA Modules:
  0.0 29.1 jit_solution(7440427097287718536)
XLA Ops:
  0.0 28.5 %nearest.1 = f32[1,512]{1,0:T(1,128)S(1)} custom-call(s32[16]{0:T(128)} %counts_hbm.1, bf16[512,1024]{1,0:T(8,128)(2,1)} %x_ref.1), custom_call_target="tpu_custom_call" | custom-call | tf_op jit(solution)/shard_map/nearest/pallas_call | solution.py:646
  28.5 0.6 %copy.4 = f32[512]{0:T(512)} copy(f32[512]{0:T(512)S(1)} %bitcast.1) | data formatting | bytes 4096

commit v2 on v1

--- a/solution.py
+++ b/solution.py
@@ -14,9 +14,10 @@
 HALF = PIECES // 2
 GROUP = 8
 
-NEAR = ((0, 1), (0, 2), (0, 3), (0, 5), (0, 6), (0, 7), (1, 2), (1, 4), (2, 3), (2, 4), (2, 6),
-        (3, 5), (3, 6), (4, 5), (4, 6), (5, 6), (5, 7), (6, 7))
-ACROSS = ((0, 0), (0, 1), (5, 0), (5, 1), (5, 4), (7, 1), (7, 2), (7, 6))
+NEAR = ((0, 1), (1, 0), (2, 3), (3, 2), (4, 5), (5, 4), (6, 7), (7, 6),
+        (0, 2), (0, 5), (0, 7), (2, 1), (2, 6), (3, 0), (4, 1), (5, 6), (6, 3), (6, 4))
+UPWARD = ((0, 0), (5, 4))
+DOWNWARD = ((6, 7),)
 MAIN_OFFSET = (-8, 1, -2, 3, 2, -5, -1, 7)
 MAIN_SLOT = (2, 0, 0, 1, 0, 1, 0, 2)
 FIRST_SEEN, LAST_SEEN = -1, 9
@@ -52,9 +53,11 @@
         return sum((role == place).astype(jnp.int32) * value for place, value in enumerate(values))
 
     barrier = pltpu.get_barrier_semaphore()
-    near_of = [[b if a == r else a for a, b in NEAR if r in (a, b)] for r in range(GROUP)]
-    up_of = [[b for a, b in ACROSS if a == r] for r in range(GROUP)]
-    down_of = [[a for a, b in ACROSS if b == r] for r in range(GROUP)]
+    def told_by(edges, r):
+        return [there for here, there in edges if here == r]
+
+    def heard_by(edges):
+        return by_role([sum(there == r for _, there in edges) for r in range(GROUP)])
 
     def greet(index):
         pl.semaphore_signal(barrier, inc=1, device_id=coords(index), device_id_type=MESH_ID)
@@ -62,22 +65,18 @@
     for r in range(GROUP):
         @pl.when(role == r)
         def _():
-            @pl.when(has_up)
-            def _():
-                for there in up_of[r]:
-                    greet(me + GROUP + there - r)
-
-            @pl.when(has_down)
-            def _():
-                for there in down_of[r]:
-                    greet(me - GROUP + there - r)
-
-            for there in near_of[r]:
+            for there in told_by(NEAR, r):
                 greet(me + there - r)
 
-    greeted = (by_role([len(n) for n in near_of])
-               + has_up.astype(jnp.int32) * by_role([len(n) for n in up_of])
-               + has_down.astype(jnp.int32) * by_role([len(n) for n in down_of]))
+            for edges, exists, step in ((UPWARD, has_up, GROUP), (DOWNWARD, has_down, -GROUP)):
+                if told_by(edges, r):
+                    @pl.when(exists)
+                    def _():
+                        for there in told_by(edges, r):
+                            greet(me + step + there - r)
+
+    greeted = (heard_by(NEAR) + has_down.astype(jnp.int32) * heard_by(UPWARD)
+               + has_up.astype(jnp.int32) * heard_by(DOWNWARD))
 
     def rows_of(q, size=piece):
         return pl.ds(pl.multiple_of(q * size, size), size)
@@ -291,26 +290,27 @@
             def _():
                 meet(left, [(main_in[2][...], same(7, 8), 4, everywhere)], 3, p, half)
 
-        @pl.loop(0, tiles)
-        def _(p):
-            both(lambda q: wait_main(0, q), p)
-            meet(main_in[0][rows_of(p, tile), :],
-                 [(own[...], same(0, 2), 0, everywhere), (main_in[1][...], same(2, 5), 2, everywhere)], 1, p)
-
+        @pl.loop(0, half_tiles)
+        def _(j):
+            @pl.loop(3 * j, 3 + j)
+            def _(p):
+                both(lambda q: wait_main(0, q), p)
+                meet(main_in[0][rows_of(p, tile), :],
+                     [(own[...], same(0, 2), 0, everywhere), (main_in[1][...], same(2, 5), 2, everywhere)], 1, p)
+
+            @pl.when(has_up)
+            def _():
+                both(lambda q: wait_half(1, q), j)
+                meet(half_in[1][rows_of(j, tile), :], [(half_in[0][...], same(7, 9), 3, high_lanes)], 5, j, half)
+
+        give(3, 7, 2)
         give(1, 2, 0)
         give(2, 5, 1)
 
         @pl.when(has_up)
         def _():
-            @pl.loop(0, half_tiles)
-            def _(p):
-                both(lambda q: wait_half(1, q), p)
-                meet(half_in[1][rows_of(p, tile), :], [(half_in[0][...], same(7, 9), 3, high_lanes)], 5, p, half)
-
             give(4, 8, 4)
             give(5, 9, 2)
-
-        give(3, 7, 2)
 
     def one_side(q):
         return side(0, q, stage.at[rows_of(q)], half_in[0].at[rows_of(q)], half_recv[0].at[q], me + 3)
@@ -338,6 +338,8 @@
         diagonal()
         from_four = same(1, 4) & jnp.logical_not(below)
 
+        wait_wide(0)
+
         @pl.loop(0, HALF)
         def _(q):
             wait_main(0, q)
@@ -351,26 +353,29 @@
                  [(own[...], same(1, 2), 0, everywhere), (other[...], same(1, 3), 2, everywhere)], 1, p)
 
         pl.loop(0, half_tiles)(first_block)
-
-        def chosen_block(p):
+        pl.loop(1, HALF)(wait_wide)
+
+        @pl.loop(0, half_tiles)
+        def _(p):
+            meet(wide_in[rows_of(p, tile), :],
+                 [(own[...], below | same(2, 4), 0, everywhere),
+                  (main_in[0][:half, :], from_four, 1, low_lanes)], 3, p)
+
+        @pl.loop(half_tiles, tiles)
+        def _(p):
+            both(lambda q: wait_main(0, q), p)
+            meet(main_in[0][rows_of(p, tile), :],
+                 [(own[...], same(1, 2), 0, everywhere), (other[...], same(1, 3), 2, everywhere),
+                  (wide_in[:half, :], from_four, 3, low_lanes)], 1, p)
+
+        give(2, 1, 0)
+
+        @pl.loop(half_tiles, tiles)
+        def _(p):
             both(wait_wide, p)
             meet(wide_in[rows_of(p, tile), :],
                  [(own[...], below | same(2, 4), 0, everywhere),
-                  (main_in[0][:half, :], from_four, 1, low_lanes)], 3, p)
-
-        pl.loop(0, half_tiles)(chosen_block)
-
-        @pl.loop(half_tiles, tiles)
-        def _(p):
-            both(lambda q: wait_main(0, q), p)
-            first_block(p)
-
-        give(2, 1, 0)
-        pl.loop(half_tiles, tiles)(chosen_block)
-
-        @pl.loop(half_tiles, tiles)
-        def _(p):
-            meet(main_in[0][rows_of(p, tile), :], [(wide_in[...], from_four, 3, everywhere)], 1, p)
+                  (main_in[0][...], from_four, 1, everywhere)], 3, p)
 
         split(3, below, 5, everywhere, 4, everywhere, everywhere)
         give(1, -1, 0)
@@ -443,7 +448,7 @@
         def _(p):
             @pl.when(has_up)
             def _():
-                @pl.loop(2 * p, 2 * p + 2)
+                @pl.loop(2 * p, 2 + p)
                 def _(i):
                     both(wait_wide, i)
                     meet(wide_in[rows_of(i, tile), :],
@@ -457,18 +462,24 @@
             def _():
                 meet(left, [(half_in[1][...], same(7, 9), 4, high_lanes)], 2, p)
 
-        give(1, 1, 0)
-
         @pl.when(has_up)
         def _():
+            early = block - tile
+
             @pl.loop(0, half_tiles)
             def _(p):
-                meet(half_in[0][rows_of(p, tile), :], [(wide_in[...], same(7, 8), 3, everywhere)], 2, p)
-
+                meet(half_in[0][rows_of(p, tile), :],
+                     [(wide_in[:early, :], same(7, 8), 3, slice(0, early))], 2, p)
+
+            both(wait_wide, tiles - 1)
+            meet(wide_in[early:, :],
+                 [(own[...], same(5, 8), 0, everywhere), (main_in[0][...], same(6, 8), 1, everywhere),
+                  (half_in[0][...], same(7, 8), 2, low_lanes)], 3, tiles - 1)
             give(3, 3, 3)
             give(4, 4, 1)
 
         give(2, 2, 1)
+        give(1, 1, 0)
 
     def six_side(q):
         return side(0, q, stage.at[rows_of(q)], wide_in.at[rows_of(q)], wide_recv.at[q], me - 4)

time: 29.4 us -> 28.7 us (0.976)
  Pallas kernels: 28.5 us -> 27.9 us
    pallas_call x1, Pallas kernels: 28.5 us -> 27.9 us  [shards(): pl.pallas_call(functools.partial(nearest_kernel, sizes), out_shape=pltpu....]
where the time goes in v2:
time: 28.7 us; the launch traced here: 28.5 us
  Pallas kernels  27.9 us (97%)
  local copies, waits for them, and re-layouts  0.58 us (2%)
    pallas_call x1, Pallas kernels, shards(): pl.pallas_call(functools.partial(nearest_kernel, sizes), out_shape=pltpu....  27.9 us
    unnamed x1, local copies, waits for them, and re-layouts  0.58 us

profile of v2, /device:TPU:1, one launch (start us, length us, event | category | flops | bytes accessed | tf_op | source)
XLA Modules:
  0.0 28.5 jit_solution(605888095377109180)
XLA Ops:
  0.0 27.9 %nearest.1 = f32[1,512]{1,0:T(1,128)S(1)} custom-call(s32[16]{0:T(128)} %counts_hbm.1, bf16[512,1024]{1,0:T(8,128)(2,1)} %x_ref.1), custom_call_target="tpu_custom_call" | custom-call | tf_op jit(solution)/shard_map/nearest/pallas_call | solution.py:657
  27.9 0.6 %copy.4 = f32[512]{0:T(512)} copy(f32[512]{0:T(512)S(1)} %bitcast.1) | data formatting | bytes 4096

commit v3 on v2

--- a/solution.py
+++ b/solution.py
@@ -10,7 +10,7 @@
 EPSILON = 1e-06
 LOW = -2.0
 MESH_ID = pl.DeviceIdType.MESH
-PIECES = 8
+PIECES = 4
 HALF = PIECES // 2
 GROUP = 8
 
@@ -37,7 +37,7 @@
     total = n_rows * n_bal
     block, width = x_ref.shape
     piece = block // PIECES
-    tile = 2 * piece
+    tile = block // 4
     half = block // 2
     me = lax.axis_index("rows") * n_bal + lax.axis_index("bal")
     role = lax.rem(me, GROUP)
@@ -223,8 +223,9 @@
         side(0, q, stage.at[rows_of(q)], half_in[slot].at[rows_of(q)], half_recv[slot].at[q], me).wait_recv()
 
     def both(wait, p):
-        wait(2 * p)
-        wait(2 * p + 1)
+        many = tile // piece
+        for k in range(many):
+            wait(many * p + k)
 
     def ret(slot, offset, place):
         return copy_to(lines[max(slot, 1)], ret_in[place], ret_send.at[slot], ret_recv.at[place], me + offset)

time: 28.7 us -> 28 us (0.976)
  Pallas kernels: 27.9 us -> 27.3 us
    pallas_call x1, Pallas kernels: 27.9 us -> 27.3 us  [shards(): pl.pallas_call(functools.partial(nearest_kernel, sizes), out_shape=pltpu....]
where the time goes in v3:
time: 28 us; the launch traced here: 27.9 us
  Pallas kernels  27.3 us (98%)
  local copies, waits for them, and re-layouts  0.58 us (2%)
    pallas_call x1, Pallas kernels, shards(): pl.pallas_call(functools.partial(nearest_kernel, sizes), out_shape=pltpu....  27.3 us
    unnamed x1, local copies, waits for them, and re-layouts  0.58 us

profile of v3, /device:TPU:1, one launch (start us, length us, event | category | flops | bytes accessed | tf_op | source)
XLA Modules:
  0.0 27.9 jit_solution(18162298977461093617)
XLA Ops:
  0.0 27.3 %nearest.1 = f32[1,512]{1,0:T(1,128)S(1)} custom-call(s32[16]{0:T(128)} %counts_hbm.1, bf16[512,1024]{1,0:T(8,128)(2,1)} %x_ref.1), custom_call_target="tpu_custom_call" | custom-call | tf_op jit(solution)/shard_map/nearest/pallas_call | solution.py:658
  27.3 0.6 %copy.4 = f32[512]{0:T(512)} copy(f32[512]{0:T(512)S(1)} %bitcast.1) | data formatting | bytes 4096

commit v4 on v3

--- a/solution.py
+++ b/solution.py
@@ -128,13 +128,14 @@
         own[rows, :] = (values * scale).astype(jnp.bfloat16)
 
     def send(q):
+        to_pair(q).start()
+
         for_main(lambda r: to_main(r, q).start())
 
         @pl.when((role == 7) & (q >= HALF))
         def _():
             high_half(q).start()
 
-        to_pair(q).start()
 
     pl.loop(0, HALF)(normalise)
     pl.semaphore_wait(barrier, greeted)

time: 28 us -> 28 us (level)
  no operation moved by 1% of the time
where the time goes in v4:
time: 28 us; the launch traced here: 27.9 us
  Pallas kernels  27.3 us (98%)
  local copies, waits for them, and re-layouts  0.58 us (2%)
    pallas_call x1, Pallas kernels, shards(): pl.pallas_call(functools.partial(nearest_kernel, sizes), out_shape=pltpu....  27.3 us
    unnamed x1, local copies, waits for them, and re-layouts  0.58 us

profile of v4, /device:TPU:1, one launch (start us, length us, event | category | flops | bytes accessed | tf_op | source)
XLA Modules:
  0.0 27.9 jit_solution(2673338266131941079)
XLA Ops:
  0.0 27.3 %nearest.1 = f32[1,512]{1,0:T(1,128)S(1)} custom-call(s32[16]{0:T(128)} %counts_hbm.1, bf16[512,1024]{1,0:T(8,128)(2,1)} %x_ref.1), custom_call_target="tpu_custom_call" | custom-call | tf_op jit(solution)/shard_map/nearest/pallas_call | solution.py:659
  27.3 0.6 %copy.4 = f32[512]{0:T(512)} copy(f32[512]{0:T(512)S(1)} %bitcast.1) | data formatting | bytes 4096
